TPU v7x, 32 devices: a whole 2x2x4 slice. The times are simulated.
32 devices in a mesh: kx: 2 (over x), ky: 4 (over y, core), kz: 4 (over z).
Axes of the slice: x: 2, y: 2, z: 4, core: 2. Of those that a mesh axis runs over, the one named last changes fastest.
Arguments:
- coefficients: bfloat16 [2, 2, 4, 4, 512, 2048], P(None, 'kx', 'ky', 'kz'), may hold values from -1 to 1
- shift_blocks: int32 [3], replicated, may hold values from 1 to 15, as said below
Outputs:
- centre: float32 [3, 512], replicated
- spread: float32 [3, 512], replicated
- coherence: float32 [3, 2, 4, 4], P(None, 'kx', 'ky', 'kz')
Inputs may be any that keep to these rules, and one draw needn't show every extreme that they name: The coefficients one period further along direction d are those of the first k-point of the string with plane-wave index g read at (g + 128 * shift_blocks[d]) mod 2048.
All inputs are finite; a program needn't handle non-finite values.
Results may differ from a plain program's by a relative error of at most 0.0003.
Values may be sent and summed in bfloat16 or wider, within the bound.
No kernel may reach another device: no remote copies, remote signals or barrier semaphores. Data moves between devices by JAX's collectives and lax.ppermute only.
A program may use at most 128 MiB of HBM per device.

v0:
```python
import jax
import jax.numpy as jnp
from jax import lax
from jax.sharding import PartitionSpec as P


def passed_along(value, axis, steps):
    count = lax.axis_size(axis)
    pairs = [(source, (source + steps) % count) for source in range(count)]
    return lax.ppermute(value, axis, pairs)


def pair_measure(own_point, partner):
    bands = own_point.shape[1]
    left_side = jnp.concatenate([own_point[0], own_point[1]], axis=1)
    right_side = jnp.concatenate(
        [
            jnp.concatenate([partner[0], partner[1]], axis=1),
            jnp.concatenate([partner[1], -partner[0]], axis=1),
        ],
        axis=0,
    )
    product = lax.dot_general(
        left_side, right_side, (((1,), (1,)), ((), ())), preferred_element_type=jnp.float32
    )
    real_part = product[:, :bands]
    imag_part = product[:, bands:]
    phases = jnp.arctan2(jnp.diagonal(imag_part), jnp.diagonal(real_part))
    coherence = jnp.sum(real_part * real_part + imag_part * imag_part) / bands
    return (phases, coherence)


def shards(coefficients, shift_blocks):
    planes = coefficients.shape[1]
    bands = coefficients.shape[4]
    width = coefficients.shape[5]
    own_planes = coefficients.reshape(2, planes, bands, width)
    shifts = shift_blocks * 128
    measure = jax.vmap(pair_measure, in_axes=(1, 1))
    next_first = passed_along(own_planes[:, 0], "kx", -1)
    x_wrap = lax.axis_index("kx") == lax.axis_size("kx") - 1
    next_first = jnp.where(x_wrap, jnp.roll(next_first, -shifts[0], axis=-1), next_first)
    x_partner = jnp.concatenate([own_planes[:, 1:], next_first[:, None]], axis=1)
    x_phases, x_coherence = measure(own_planes, x_partner)
    later = passed_along(own_planes, "ky", -1)
    y_wrap = lax.axis_index("ky") == lax.axis_size("ky") - 1
    y_partner = jnp.where(y_wrap, jnp.roll(later, -shifts[1], axis=-1), later)
    y_phases, y_coherence = measure(own_planes, y_partner)
    z_later = passed_along(own_planes, "kz", -1)
    z_wrap = lax.axis_index("kz") == lax.axis_size("kz") - 1
    z_partner = jnp.where(z_wrap, jnp.roll(z_later, -shifts[2], axis=-1), z_later)
    z_phases, z_coherence = measure(own_planes, z_partner)
    phases = jnp.stack([x_phases, y_phases, z_phases])
    coherence = jnp.stack([x_coherence, y_coherence, z_coherence]).reshape(3, planes, 1, 1)
    k_total = planes * lax.axis_size("kx") * lax.axis_size("ky") * lax.axis_size("kz")
    counts = jnp.array(
        [planes * lax.axis_size("kx"), lax.axis_size("ky"), lax.axis_size("kz")], jnp.float32
    )
    phase_sum = jnp.sum(phases, axis=1)
    totals, squares = lax.psum((phase_sum, jnp.sum(phases * phases, axis=1)), ("kx", "ky", "kz"))
    mean_phase = totals / k_total
    variance = squares / k_total - mean_phase * mean_phase
    centre = -counts[:, None] * mean_phase / (2.0 * jnp.pi)
    spread = (counts[:, None] / (2.0 * jnp.pi)) ** 2 * variance
    return (centre, spread, coherence)


def solution(mesh):
    in_specs = (P(None, "kx", "ky", "kz", None, None), P())
    out_specs = (P(), P(), P(None, "kx", "ky", "kz"))
    return jax.shard_map(shards, mesh=mesh, in_specs=in_specs, out_specs=out_specs, check_vma=False)
```

profile of v0, /device:TPU:0, one launch (start us, length us, event | category | flops | bytes accessed | tf_op | source)
XLA Modules:
  0.0 244.8 jit_solution(3515584299984125351)
XLA Ops:
  0.6 5.1 %collective-permute-start.2 = (bf16[2,1,512,2048]{3,2,0,1:T(8,128)(2,1)}, bf16[2,1,512,2048]{3,2,0,1:T(8,128)(2,1)}, u32[]{:S(2)}, u32[]{:S(2)}) collective-permute-start(bf16[2,1,512,2048]{3,2,0,1:T(8,128)(2,1)} %bitcast.83), channel_id=1, source_target_pairs={{0,3},{1,0},{2,1},{3,2},{4,7},{5,4},{6,5},{7,6},{8,11},{9,8},{10,9... | collective-permute-start | bytes 12582920 | tf_op jit(solution)/shard_map/ppermute | solution.py:10
  5.8 0.7 collective-permute-start.1
  6.4 1.5 collective-permute-start
  7.9 0.7 broadcast_multiply_fusion
  8.6 0.6 fusion.36
  11.9 4.8 %slice_bitcast_fusion.5 = (bf16[1,512,2048]{2,1,0:T(8,128)(2,1)}, bf16[1,512,2048]{2,1,0:T(8,128)(2,1)}) fusion(bf16[2,1,1,1,512,2048]{5,4,3,2,1,0:T(8,128)(2,1)} %param.5), kind=kLoop, calls=%fused_computation.48 | loop fusion | bytes 8388608 | tf_op jit(solution)/shard_map/vmap()/squeeze;vmap()/transpose | solution.py:15
  16.6 79.3 %collective-permute-done.2 = bf16[2,1,512,2048]{3,2,0,1:T(8,128)(2,1)} collective-permute-done((bf16[2,1,512,2048]{3,2,0,1:T(8,128)(2,1)}, bf16[2,1,512,2048]{3,2,0,1:T(8,128)(2,1)}, u32[]{:S(2)}, u32[]{:S(2)}) %collective-permute-start.2) | collective-permute-done | bytes 4194336 | tf_op jit(solution)/shard_map/ppermute | solution.py:10
  95.9 6.5 %fusion.38 = bf16[2,1,512,2048]{3,2,1,0:T(8,128)(2,1)S(1)} fusion(bf16[2,1,512,2048]{3,2,0,1:T(8,128)(2,1)} %collective-permute-done.2, s32[]{:T(128)S(6)} %select_n.69, pred[]{:T(512)S(6)} %eq.15), kind=kLoop, calls=%fused_computation.77 | loop fusion | flops 10485760 | bytes 8388613 | tf_op jit(solution)/shard_map/jit(_where)/select_n | solution.py:51
  102.4 1.5 fusion.34
  103.8 1.6 slice_bitcast_fusion.1
  105.4 0.0 collective-permute-done.1
  105.4 7.6 %fusion.37 = bf16[2,1,512,2048]{3,2,1,0:T(8,128)(2,1)S(1)} fusion(bf16[2,1,512,2048]{3,2,0,1:T(8,128)(2,1)} %collective-permute-done.1, s32[]{:T(128)S(6)} %select_n.67, pred[]{:T(512)S(6)} %eq.14), kind=kLoop, calls=%fused_computation.76 | loop fusion | flops 10485760 | bytes 8388613 | tf_op jit(solution)/shard_map/jit(_where)/select_n | solution.py:47
  113.0 1.5 fusion.33
  114.5 1.5 slice_bitcast_fusion.3
  116.0 0.0 collective-permute-done
  116.0 6.5 %fusion.26 = bf16[2,512,2048]{2,1,0:T(8,128)(2,1)S(1)} fusion(bf16[2,512,2048]{2,1,0:T(8,128)(2,1)} %collective-permute-done, s32[]{:T(128)S(6)} %select_n.58, pred[]{:T(512)S(6)} %eq.13), kind=kLoop, calls=%fused_computation.41 | loop fusion | flops 10485760 | bytes 8388613 | tf_op jit(solution)/shard_map/jit(_where)/select_n | solution.py:42
  122.5 0.4 fusion.35
  122.9 8.1 %fusion.29 = f32[1,512,1024]{2,1,0:T(8,128)} fusion(bf16[1,512,2048]{2,1,0:T(8,128)(2,1)S(1)} %get-tuple-element.7, bf16[1,512,2048]{2,1,0:T(8,128)(2,1)S(1)} %get-tuple-element.8, bf16[1,512,2048]{2,1,0:T(8,128)(2,1)S(1)} %get-tuple-element.6, bf16[1,512,2048]{2,1,0:T(8,128)(2,1)} %get-tuple-element.10, bf16[1,512,2048]{2,1,0:T(8,128)(2,1)} %get-tuple-element.9), kind=kOutput, calls=%fused_computation.51 | convolution fusion | flops 4336910336 | bytes 12582912 | tf_op jit(solution)/shard_map/vmap()/dot_general | solution.py:23
  131.0 2.5 %add_reduce_fusion.2 = (f32[]{:T(128)}, f32[512,512]{1,0:T(8,128)S(1)}, f32[512,512]{1,0:T(8,128)S(1)}) fusion(f32[1,512,1024]{2,1,0:T(8,128)} %fusion.29), kind=kLoop, calls=%fused_computation.54 | loop fusion | flops 1048575 | bytes 4194308 | tf_op jit(solution)/shard_map/vmap()/reduce_sum | solution.py:29
  133.5 4.5 %gather_fusion.1 = f32[512]{0:T(512)S(1)} fusion(f32[512,512]{1,0:T(8,128)S(1)} %get-tuple-element.12, s32[512]{0:T(512)S(1)} %bitcast.77), kind=kCustom, calls=%fused_computation.1 | custom fusion | bytes 8192 | tf_op jit(solution)/shard_map/vmap(jit(diagonal))/cond/branch_0_fun/gather | solution.py:28
  138.1 4.5 %gather_fusion = f32[512]{0:T(512)S(1)} fusion(f32[512,512]{1,0:T(8,128)S(1)} %get-tuple-element.13, s32[512]{0:T(512)S(1)} %bitcast.78), kind=kCustom, calls=%fused_computation | custom fusion | bytes 8192 | tf_op jit(solution)/shard_map/vmap(jit(diagonal))/cond/branch_0_fun/gather | solution.py:28
  142.6 6.5 %fusion.22 = bf16[2,1,512,2048]{3,2,0,1:T(8,128)(2,1)S(1)} fusion(bf16[2,1,512,2048]{3,2,0,1:T(8,128)(2,1)} %collective-permute-done.2, s32[]{:T(128)S(6)} %select_n.69, pred[]{:T(512)S(6)} %eq.15), kind=kLoop, calls=%fused_computation.37 | loop fusion | flops 10485760 | bytes 8388613 | tf_op jit(solution)/shard_map/jit(_where)/select_n | solution.py:51
  149.1 0.0 copy-start.2
  149.1 0.0 copy-start.3
  149.1 0.1 slice_bitcast_fusion
  149.2 1.4 copy-done.2
  150.7 0.6 copy-done.3
  151.3 8.1 %fusion.27 = f32[1,512,1024]{2,1,0:T(8,128)} fusion(bf16[1,512,2048]{2,1,0:T(8,128)(2,1)S(1)} %copy-done.2, bf16[1,512,2048]{2,1,0:T(8,128)(2,1)S(1)} %slice_bitcast_fusion, bf16[1,512,2048]{2,1,0:T(8,128)(2,1)S(1)} %copy-done.3, bf16[1,512,2048]{2,1,0:T(8,128)(2,1)} %get-tuple-element.10, bf16[1,512,2048]{2,1,0:T(8,128)(2,1)} %get-tuple-element.9), kind=kOutput, calls=%fused_computation.49 | convolution fusion | flops 4336910336 | bytes 12582912 | tf_op jit(solution)/shard_map/vmap()/dot_general | solution.py:23
  159.4 2.5 %add_reduce_fusion = (f32[]{:T(128)}, f32[512,512]{1,0:T(8,128)S(1)}, f32[512,512]{1,0:T(8,128)S(1)}) fusion(f32[1,512,1024]{2,1,0:T(8,128)} %fusion.27), kind=kLoop, calls=%fused_computation.52 | loop fusion | flops 1048575 | bytes 4194308 | tf_op jit(solution)/shard_map/vmap()/reduce_sum | solution.py:29
  163.2 4.5 %gather_fusion.5 = f32[512]{0:T(512)S(1)} fusion(f32[512,512]{1,0:T(8,128)S(1)} %get-tuple-element.18, s32[512]{0:T(512)S(1)} %bitcast.79), kind=kCustom, calls=%fused_computation.5 | custom fusion | bytes 8192 | tf_op jit(solution)/shard_map/vmap(jit(diagonal))/cond/branch_0_fun/gather | solution.py:28
  167.7 4.5 %gather_fusion.4 = f32[512]{0:T(512)S(1)} fusion(f32[512,512]{1,0:T(8,128)S(1)} %get-tuple-element.19, s32[512]{0:T(512)S(1)} %bitcast.80), kind=kCustom, calls=%fused_computation.4 | custom fusion | bytes 8192 | tf_op jit(solution)/shard_map/vmap(jit(diagonal))/cond/branch_0_fun/gather | solution.py:28
  172.2 7.8 %fusion.24 = bf16[2,1,512,2048]{3,2,0,1:T(8,128)(2,1)S(1)} fusion(bf16[2,1,512,2048]{3,2,0,1:T(8,128)(2,1)} %collective-permute-done.1, s32[]{:T(128)S(6)} %select_n.67, pred[]{:T(512)S(6)} %eq.14), kind=kLoop, calls=%fused_computation.39 | loop fusion | flops 10485760 | bytes 8388613 | tf_op jit(solution)/shard_map/jit(_where)/select_n | solution.py:47
  180.0 0.0 copy-start
  180.0 0.0 copy-start.1
  180.1 0.1 slice_bitcast_fusion.2
  180.2 1.4 copy-done
  181.6 0.6 copy-done.1
  182.3 8.1 %fusion.28 = f32[1,512,1024]{2,1,0:T(8,128)} fusion(bf16[1,512,2048]{2,1,0:T(8,128)(2,1)S(1)} %copy-done, bf16[1,512,2048]{2,1,0:T(8,128)(2,1)S(1)} %slice_bitcast_fusion.2, bf16[1,512,2048]{2,1,0:T(8,128)(2,1)S(1)} %copy-done.1, bf16[1,512,2048]{2,1,0:T(8,128)(2,1)} %get-tuple-element.10, bf16[1,512,2048]{2,1,0:T(8,128)(2,1)} %get-tuple-element.9), kind=kOutput, calls=%fused_computation.50 | convolution fusion | flops 4336910336 | bytes 12582912 | tf_op jit(solution)/shard_map/vmap()/dot_general | solution.py:23
  190.4 0.0 copy-start.4
  190.4 0.0 copy-start.5
  190.4 2.5 %add_reduce_fusion.1 = (f32[]{:T(128)}, f32[512,512]{1,0:T(8,128)S(1)}, f32[512,512]{1,0:T(8,128)S(1)}) fusion(f32[1,512,1024]{2,1,0:T(8,128)} %fusion.28), kind=kLoop, calls=%fused_computation.53 | loop fusion | flops 1048575 | bytes 4194308 | tf_op jit(solution)/shard_map/vmap()/reduce_sum | solution.py:29
  193.5 4.5 %gather_fusion.3 = f32[512]{0:T(512)S(1)} fusion(f32[512,512]{1,0:T(8,128)S(1)} %get-tuple-element.15, s32[512]{0:T(512)S(1)} %bitcast.81), kind=kCustom, calls=%fused_computation.3 | custom fusion | bytes 8192 | tf_op jit(solution)/shard_map/vmap(jit(diagonal))/cond/branch_0_fun/gather | solution.py:28
  198.1 4.5 %gather_fusion.2 = f32[512]{0:T(512)S(1)} fusion(f32[512,512]{1,0:T(8,128)S(1)} %get-tuple-element.16, s32[512]{0:T(512)S(1)} %bitcast.82), kind=kCustom, calls=%fused_computation.2 | custom fusion | bytes 8192 | tf_op jit(solution)/shard_map/vmap(jit(diagonal))/cond/branch_0_fun/gather | solution.py:28
  202.8 40.7 %all-reduce = (f32[3,512]{1,0:T(4,128)S(1)}, f32[3,512]{1,0:T(4,128)S(1)}) all-reduce(f32[3,512]{1,0:T(4,128)S(1)} %maximum_bitcast_fusion.16, f32[3,512]{1,0:T(4,128)S(1)} %maximum_multiply_fusion), channel_id=1, replica_groups=mesh['kx'=2,'ky'=4,'kz'=4] {'kx','ky','kz'}, use_global_device_ids=true, to_apply=%region_0.2 | all-reduce | flops 3072 | bytes 24576 | tf_op jit(solution)/shard_map/psum | solution.py:60
  243.5 0.6 maximum_bitcast_fusion.17
  244.1 0.0 copy-done.4
  244.1 0.0 copy-done.5
  244.1 0.7 subtract_multiply_fusion
  (6 shorter events, 0.1 us)
Async XLA Ops:
  0.6 95.3 %collective-permute-start.2 = (bf16[2,1,512,2048]{3,2,0,1:T(8,128)(2,1)}, bf16[2,1,512,2048]{3,2,0,1:T(8,128)(2,1)}, u32[]{:S(2)}, u32[]{:S(2)}) collective-permute-start(bf16[2,1,512,2048]{3,2,0,1:T(8,128)(2,1)} %bitcast.83), channel_id=1, source_target_pairs={{0,3},{1,0},{2,1},{3,2},{4,7},{5,4},{6,5},{7,6},{8,11},{9,8},{10,9... | collective-permute-start | bytes 12582920 | tf_op jit(solution)/shard_map/ppermute | solution.py:10
  5.8 99.7 %collective-permute-start.1 = (bf16[2,1,512,2048]{3,2,0,1:T(8,128)(2,1)}, bf16[2,1,512,2048]{3,2,0,1:T(8,128)(2,1)}, u32[]{:S(2)}, u32[]{:S(2)}) collective-permute-start(bf16[2,1,512,2048]{3,2,0,1:T(8,128)(2,1)} %bitcast.84), channel_id=1, source_target_pairs={{0,12},{4,0},{8,4},{12,8},{1,13},{5,1},{9,5},{13,9},{2,14},{6,2},{... | collective-permute-start | bytes 12582920 | tf_op jit(solution)/shard_map/ppermute | solution.py:10
  6.4 109.6 %collective-permute-start = (bf16[2,512,2048]{2,1,0:T(8,128)(2,1)}, bf16[2,512,2048]{2,1,0:T(8,128)(2,1)}, u32[]{:S(2)}, u32[]{:S(2)}) collective-permute-start(bf16[2,512,2048]{2,1,0:T(8,128)(2,1)} %bitcast.85), channel_id=1, source_target_pairs={{0,16},{16,0},{1,17},{17,1},{2,18},{18,2},{3,19},{19,3},{4,20},{20... | collective-permute-start | bytes 12582920 | tf_op jit(solution)/shard_map/ppermute | solution.py:10
  149.1 1.6 copy-start.2
  149.1 2.2 copy-start.3
  180.0 1.6 copy-start
  180.0 2.2 copy-start.1
  190.4 53.7 %copy-start.4 = (f32[3]{0:T(128)S(1)}, f32[3]{0:T(128)}, u32[]{:S(2)}) copy-start(f32[3]{0:T(128)} %constant.98) | copy-start | bytes 40
  190.4 53.7 %copy-start.5 = (f32[3]{0:T(128)S(1)}, f32[3]{0:T(128)}, u32[]{:S(2)}) copy-start(f32[3]{0:T(128)} %constant.95) | copy-start | bytes 40
where the time goes:
time: 245 us
  waiting for transfers between devices  79.3 us (32%)
  other arithmetic  47.5 us (19%)
  blocking collectives  40.7 us (17%)
  local copies, waits for them, and re-layouts  40.1 us (16%)
  matrix products  24.3 us (10%)
  starting transfers between devices  7.3 us (3%)
  between operations  5.43 us (2%)
    ppermute x3, waiting for transfers between devices, passed_along(): return lax.ppermute(value, axis, pairs)  79.3 us
    psum x1, blocking collectives, shards(): lax.psum((phase_sum, jnp.sum(phases * phases, axis=1)), ('kx', 'ky', 'kz'))  40.7 us
    gather x6, local copies, waits for them, and re-layouts, pair_measure(): phases = jnp.arctan2(jnp.diagonal(imag_part), jnp.diagonal(real_part))  27.1 us
    dot_general x3, matrix products, pair_measure(): lax.dot_general(left_side, right_side, (((1,), (1,)), ((), ())), preferre...  24.3 us
    select_n x2, other arithmetic, shards(): y_partner = jnp.where(y_wrap, jnp.roll(later, -shifts[1], axis=-1), later)  15.3 us
    select_n x2, other arithmetic, shards(): jnp.where(z_wrap, jnp.roll(z_later, -shifts[2], axis=-1), z_later)  12.9 us
    reduce_sum x3, other arithmetic, pair_measure(): coherence = jnp.sum(real_part * real_part + imag_part * imag_part) / bands  7.5 us
    ppermute x3, starting transfers between devices, passed_along(): return lax.ppermute(value, axis, pairs)  7.3 us
  transfers between devices with their start and end apart: 3, of which 1 were waited for; matrix products, arithmetic and copies ran while one was open for 11% of the time, Pallas kernels for 0%

commit v1 on v0

--- a/solution.py
+++ b/solution.py
@@ -57,7 +57,12 @@
         [planes * lax.axis_size("kx"), lax.axis_size("ky"), lax.axis_size("kz")], jnp.float32
     )
     phase_sum = jnp.sum(phases, axis=1)
-    totals, squares = lax.psum((phase_sum, jnp.sum(phases * phases, axis=1)), ("kx", "ky", "kz"))
+    cover_strips_all = lambda page, shard_axis, mesh_ax: jax.lax.psum(
+        jax.lax.psum(page, shard_axis), mesh_ax
+    )
+    totals, squares = cover_strips_all(
+        (phase_sum, jnp.sum(phases * phases, axis=1)), ("ky", "kz"), "kx"
+    )
     mean_phase = totals / k_total
     variance = squares / k_total - mean_phase * mean_phase
     centre = -counts[:, None] * mean_phase / (2.0 * jnp.pi)

time: 245 us -> 274 us (1.12)
  blocking collectives: 40.7 us -> 69.8 us
    psum x1 -> x2, blocking collectives: 40.7 us -> 69.8 us  [the longest x1 61.7 us: shards(): jax.lax.psum(page, shard_axis)]
  transfers between devices with their start and end apart: 3 -> 3, of which waited for: 1 -> 1; matrix products, arithmetic and copies ran while one was open for 11% -> 10% of each run, Pallas kernels for 0% -> 0%
where the time goes in v1:
time: 274 us
  waiting for transfers between devices  79.3 us (29%)
  blocking collectives  69.8 us (25%)
  other arithmetic  47.4 us (17%)
  local copies, waits for them, and re-layouts  40.1 us (15%)
  matrix products  24.3 us (9%)
  starting transfers between devices  7.3 us (3%)
  between operations  5.43 us (2%)
    ppermute x3, waiting for transfers between devices, passed_along(): return lax.ppermute(value, axis, pairs)  79.3 us
    psum x1, blocking collectives, shards(): jax.lax.psum(page, shard_axis)  61.7 us
    gather x6, local copies, waits for them, and re-layouts, pair_measure(): phases = jnp.arctan2(jnp.diagonal(imag_part), jnp.diagonal(real_part))  27.1 us
    dot_general x3, matrix products, pair_measure(): lax.dot_general(left_side, right_side, (((1,), (1,)), ((), ())), preferre...  24.3 us
    select_n x2, other arithmetic, shards(): y_partner = jnp.where(y_wrap, jnp.roll(later, -shifts[1], axis=-1), later)  15.2 us
    select_n x2, other arithmetic, shards(): jnp.where(z_wrap, jnp.roll(z_later, -shifts[2], axis=-1), z_later)  12.9 us
    psum x1, blocking collectives, shards(): jax.lax.psum(jax.lax.psum(page, shard_axis), mesh_ax)  8.08 us
    reduce_sum x3, other arithmetic, pair_measure(): coherence = jnp.sum(real_part * real_part + imag_part * imag_part) / bands  7.5 us
  transfers between devices with their start and end apart: 3, of which 1 were waited for; matrix products, arithmetic and copies ran while one was open for 10% of the time, Pallas kernels for 0%

profile of v1, /device:TPU:0, one launch (start us, length us, event | category | flops | bytes accessed | tf_op | source)
XLA Modules:
  0.0 273.6 jit_solution(15502830539365730436)
XLA Ops:
  0.6 5.1 %collective-permute-start.2 = (bf16[2,1,512,2048]{3,2,0,1:T(8,128)(2,1)}, bf16[2,1,512,2048]{3,2,0,1:T(8,128)(2,1)}, u32[]{:S(2)}, u32[]{:S(2)}) collective-permute-start(bf16[2,1,512,2048]{3,2,0,1:T(8,128)(2,1)} %bitcast.83), channel_id=1, source_target_pairs={{0,3},{1,0},{2,1},{3,2},{4,7},{5,4},{6,5},{7,6},{8,11},{9,8},{10,9... | collective-permute-start | bytes 12582920 | tf_op jit(solution)/shard_map/ppermute | solution.py:10
  5.8 0.7 collective-permute-start.1
  6.4 1.5 collective-permute-start
  7.9 0.7 broadcast_multiply_fusion
  8.6 0.6 fusion.36
  11.9 4.7 %slice_bitcast_fusion.5 = (bf16[1,512,2048]{2,1,0:T(8,128)(2,1)}, bf16[1,512,2048]{2,1,0:T(8,128)(2,1)}) fusion(bf16[2,1,1,1,512,2048]{5,4,3,2,1,0:T(8,128)(2,1)} %param.5), kind=kLoop, calls=%fused_computation.48 | loop fusion | bytes 8388608 | tf_op jit(solution)/shard_map/vmap()/squeeze;vmap()/transpose | solution.py:15
  16.6 79.3 %collective-permute-done.2 = bf16[2,1,512,2048]{3,2,0,1:T(8,128)(2,1)} collective-permute-done((bf16[2,1,512,2048]{3,2,0,1:T(8,128)(2,1)}, bf16[2,1,512,2048]{3,2,0,1:T(8,128)(2,1)}, u32[]{:S(2)}, u32[]{:S(2)}) %collective-permute-start.2) | collective-permute-done | bytes 4194336 | tf_op jit(solution)/shard_map/ppermute | solution.py:10
  95.9 6.5 %fusion.38 = bf16[2,1,512,2048]{3,2,1,0:T(8,128)(2,1)S(1)} fusion(bf16[2,1,512,2048]{3,2,0,1:T(8,128)(2,1)} %collective-permute-done.2, s32[]{:T(128)S(6)} %select_n.69, pred[]{:T(512)S(6)} %eq.15), kind=kLoop, calls=%fused_computation.77 | loop fusion | flops 10485760 | bytes 8388613 | tf_op jit(solution)/shard_map/jit(_where)/select_n | solution.py:51
  102.4 1.4 fusion.34
  103.8 1.6 slice_bitcast_fusion.1
  105.4 0.0 collective-permute-done.1
  105.4 7.5 %fusion.37 = bf16[2,1,512,2048]{3,2,1,0:T(8,128)(2,1)S(1)} fusion(bf16[2,1,512,2048]{3,2,0,1:T(8,128)(2,1)} %collective-permute-done.1, s32[]{:T(128)S(6)} %select_n.67, pred[]{:T(512)S(6)} %eq.14), kind=kLoop, calls=%fused_computation.76 | loop fusion | flops 10485760 | bytes 8388613 | tf_op jit(solution)/shard_map/jit(_where)/select_n | solution.py:47
  112.9 1.5 fusion.33
  114.4 1.6 slice_bitcast_fusion.3
  115.9 0.0 collective-permute-done
  115.9 6.5 %fusion.26 = bf16[2,512,2048]{2,1,0:T(8,128)(2,1)S(1)} fusion(bf16[2,512,2048]{2,1,0:T(8,128)(2,1)} %collective-permute-done, s32[]{:T(128)S(6)} %select_n.58, pred[]{:T(512)S(6)} %eq.13), kind=kLoop, calls=%fused_computation.41 | loop fusion | flops 10485760 | bytes 8388613 | tf_op jit(solution)/shard_map/jit(_where)/select_n | solution.py:42
  122.4 0.4 fusion.35
  122.8 8.1 %fusion.29 = f32[1,512,1024]{2,1,0:T(8,128)} fusion(bf16[1,512,2048]{2,1,0:T(8,128)(2,1)S(1)} %get-tuple-element.9, bf16[1,512,2048]{2,1,0:T(8,128)(2,1)S(1)} %get-tuple-element.10, bf16[1,512,2048]{2,1,0:T(8,128)(2,1)S(1)} %get-tuple-element.8, bf16[1,512,2048]{2,1,0:T(8,128)(2,1)} %get-tuple-element.12, bf16[1,512,2048]{2,1,0:T(8,128)(2,1)} %get-tuple-element.11), kind=kOutput, calls=%fused_computation.51 | convolution fusion | flops 4336910336 | bytes 12582912 | tf_op jit(solution)/shard_map/vmap()/dot_general | solution.py:23
  130.9 2.5 add_reduce_fusion.2
  133.4 4.5 %gather_fusion.1 = f32[512]{0:T(512)S(1)} fusion(f32[512,512]{1,0:T(8,128)S(1)} %get-tuple-element.14, s32[512]{0:T(512)S(1)} %bitcast.77), kind=kCustom, calls=%fused_computation.1 | custom fusion | bytes 8192 | tf_op jit(solution)/shard_map/vmap(jit(diagonal))/cond/branch_0_fun/gather | solution.py:28
  138.0 4.5 %gather_fusion = f32[512]{0:T(512)S(1)} fusion(f32[512,512]{1,0:T(8,128)S(1)} %get-tuple-element.15, s32[512]{0:T(512)S(1)} %bitcast.78), kind=kCustom, calls=%fused_computation | custom fusion | bytes 8192 | tf_op jit(solution)/shard_map/vmap(jit(diagonal))/cond/branch_0_fun/gather | solution.py:28
  142.5 6.5 %fusion.22 = bf16[2,1,512,2048]{3,2,0,1:T(8,128)(2,1)S(1)} fusion(bf16[2,1,512,2048]{3,2,0,1:T(8,128)(2,1)} %collective-permute-done.2, s32[]{:T(128)S(6)} %select_n.69, pred[]{:T(512)S(6)} %eq.15), kind=kLoop, calls=%fused_computation.37 | loop fusion | flops 10485760 | bytes 8388613 | tf_op jit(solution)/shard_map/jit(_where)/select_n | solution.py:51
  149.0 0.0 copy-start.2
  149.0 0.0 copy-start.3
  149.0 0.1 slice_bitcast_fusion
  149.1 1.4 copy-done.2
  150.6 0.6 copy-done.3
  151.2 8.1 %fusion.27 = f32[1,512,1024]{2,1,0:T(8,128)} fusion(bf16[1,512,2048]{2,1,0:T(8,128)(2,1)S(1)} %copy-done.2, bf16[1,512,2048]{2,1,0:T(8,128)(2,1)S(1)} %slice_bitcast_fusion, bf16[1,512,2048]{2,1,0:T(8,128)(2,1)S(1)} %copy-done.3, bf16[1,512,2048]{2,1,0:T(8,128)(2,1)} %get-tuple-element.12, bf16[1,512,2048]{2,1,0:T(8,128)(2,1)} %get-tuple-element.11), kind=kOutput, calls=%fused_computation.49 | convolution fusion | flops 4336910336 | bytes 12582912 | tf_op jit(solution)/shard_map/vmap()/dot_general | solution.py:23
  159.3 2.5 add_reduce_fusion
  163.1 4.5 %gather_fusion.5 = f32[512]{0:T(512)S(1)} fusion(f32[512,512]{1,0:T(8,128)S(1)} %get-tuple-element.20, s32[512]{0:T(512)S(1)} %bitcast.79), kind=kCustom, calls=%fused_computation.5 | custom fusion | bytes 8192 | tf_op jit(solution)/shard_map/vmap(jit(diagonal))/cond/branch_0_fun/gather | solution.py:28
  167.6 4.5 %gather_fusion.4 = f32[512]{0:T(512)S(1)} fusion(f32[512,512]{1,0:T(8,128)S(1)} %get-tuple-element.21, s32[512]{0:T(512)S(1)} %bitcast.80), kind=kCustom, calls=%fused_computation.4 | custom fusion | bytes 8192 | tf_op jit(solution)/shard_map/vmap(jit(diagonal))/cond/branch_0_fun/gather | solution.py:28
  172.1 7.7 %fusion.24 = bf16[2,1,512,2048]{3,2,0,1:T(8,128)(2,1)S(1)} fusion(bf16[2,1,512,2048]{3,2,0,1:T(8,128)(2,1)} %collective-permute-done.1, s32[]{:T(128)S(6)} %select_n.67, pred[]{:T(512)S(6)} %eq.14), kind=kLoop, calls=%fused_computation.39 | loop fusion | flops 10485760 | bytes 8388613 | tf_op jit(solution)/shard_map/jit(_where)/select_n | solution.py:47
  179.9 0.0 copy-start
  179.9 0.0 copy-start.1
  179.9 0.1 slice_bitcast_fusion.2
  180.0 1.4 copy-done
  181.4 0.6 copy-done.1
  182.1 8.1 %fusion.28 = f32[1,512,1024]{2,1,0:T(8,128)} fusion(bf16[1,512,2048]{2,1,0:T(8,128)(2,1)S(1)} %copy-done, bf16[1,512,2048]{2,1,0:T(8,128)(2,1)S(1)} %slice_bitcast_fusion.2, bf16[1,512,2048]{2,1,0:T(8,128)(2,1)S(1)} %copy-done.1, bf16[1,512,2048]{2,1,0:T(8,128)(2,1)} %get-tuple-element.12, bf16[1,512,2048]{2,1,0:T(8,128)(2,1)} %get-tuple-element.11), kind=kOutput, calls=%fused_computation.50 | convolution fusion | flops 4336910336 | bytes 12582912 | tf_op jit(solution)/shard_map/vmap()/dot_general | solution.py:23
  190.2 0.0 copy-start.4
  190.2 2.5 add_reduce_fusion.1
  193.3 4.5 %gather_fusion.3 = f32[512]{0:T(512)S(1)} fusion(f32[512,512]{1,0:T(8,128)S(1)} %get-tuple-element.17, s32[512]{0:T(512)S(1)} %bitcast.81), kind=kCustom, calls=%fused_computation.3 | custom fusion | bytes 8192 | tf_op jit(solution)/shard_map/vmap(jit(diagonal))/cond/branch_0_fun/gather | solution.py:28
  197.9 4.5 %gather_fusion.2 = f32[512]{0:T(512)S(1)} fusion(f32[512,512]{1,0:T(8,128)S(1)} %get-tuple-element.18, s32[512]{0:T(512)S(1)} %bitcast.82), kind=kCustom, calls=%fused_computation.2 | custom fusion | bytes 8192 | tf_op jit(solution)/shard_map/vmap(jit(diagonal))/cond/branch_0_fun/gather | solution.py:28
  202.6 61.7 %all-reduce = (f32[3,512]{1,0:T(4,128)S(1)}, f32[3,512]{1,0:T(4,128)S(1)}) all-reduce(f32[3,512]{1,0:T(4,128)S(1)} %maximum_bitcast_fusion.16, f32[3,512]{1,0:T(4,128)S(1)} %maximum_multiply_fusion), channel_id=1, replica_groups=mesh['kx'=2,'ky'=4,'kz'=4] {'ky','kz'}, use_global_device_ids=true, to_apply=%region_0.2 | all-reduce | flops 3072 | bytes 24576 | tf_op jit(solution)/shard_map/psum | solution.py:61
  264.3 8.1 %all-reduce.1 = (f32[3,512]{1,0:T(4,128)S(1)}, f32[3,512]{1,0:T(4,128)S(1)}) all-reduce(f32[3,512]{1,0:T(4,128)S(1)} %get-tuple-element.4, f32[3,512]{1,0:T(4,128)S(1)} %get-tuple-element.5), channel_id=1, replica_groups=mesh['kx'=2,'ky'=4,'kz'=4] {'kx'}, use_global_device_ids=true, to_apply=%region_1.3 | all-reduce | flops 3072 | bytes 24576 | tf_op jit(solution)/shard_map/psum | solution.py:60
  272.4 0.6 maximum_bitcast_fusion.17
  272.9 0.0 copy-done.4
  272.9 0.0 copy-done.5
  272.9 0.7 subtract_multiply_fusion
  (7 shorter events, 0.1 us)
Async XLA Ops:
  0.6 95.3 %collective-permute-start.2 = (bf16[2,1,512,2048]{3,2,0,1:T(8,128)(2,1)}, bf16[2,1,512,2048]{3,2,0,1:T(8,128)(2,1)}, u32[]{:S(2)}, u32[]{:S(2)}) collective-permute-start(bf16[2,1,512,2048]{3,2,0,1:T(8,128)(2,1)} %bitcast.83), channel_id=1, source_target_pairs={{0,3},{1,0},{2,1},{3,2},{4,7},{5,4},{6,5},{7,6},{8,11},{9,8},{10,9... | collective-permute-start | bytes 12582920 | tf_op jit(solution)/shard_map/ppermute | solution.py:10
  5.8 99.7 %collective-permute-start.1 = (bf16[2,1,512,2048]{3,2,0,1:T(8,128)(2,1)}, bf16[2,1,512,2048]{3,2,0,1:T(8,128)(2,1)}, u32[]{:S(2)}, u32[]{:S(2)}) collective-permute-start(bf16[2,1,512,2048]{3,2,0,1:T(8,128)(2,1)} %bitcast.84), channel_id=1, source_target_pairs={{0,12},{4,0},{8,4},{12,8},{1,13},{5,1},{9,5},{13,9},{2,14},{6,2},{... | collective-permute-start | bytes 12582920 | tf_op jit(solution)/shard_map/ppermute | solution.py:10
  6.4 109.5 %collective-permute-start = (bf16[2,512,2048]{2,1,0:T(8,128)(2,1)}, bf16[2,512,2048]{2,1,0:T(8,128)(2,1)}, u32[]{:S(2)}, u32[]{:S(2)}) collective-permute-start(bf16[2,512,2048]{2,1,0:T(8,128)(2,1)} %bitcast.85), channel_id=1, source_target_pairs={{0,16},{16,0},{1,17},{17,1},{2,18},{18,2},{3,19},{19,3},{4,20},{20... | collective-permute-start | bytes 12582920 | tf_op jit(solution)/shard_map/ppermute | solution.py:10
  149.0 1.6 copy-start.2
  149.0 2.2 copy-start.3
  179.9 1.6 copy-start
  179.9 2.2 copy-start.1
  190.2 82.8 %copy-start.4 = (f32[3]{0:T(128)S(1)}, f32[3]{0:T(128)}, u32[]{:S(2)}) copy-start(f32[3]{0:T(128)} %constant.98) | copy-start | bytes 40
  190.2 82.8 %copy-start.5 = (f32[3]{0:T(128)S(1)}, f32[3]{0:T(128)}, u32[]{:S(2)}) copy-start(f32[3]{0:T(128)} %constant.95) | copy-start | bytes 40
